TPU v7x, 32 devices: a whole 2x2x4 slice. The times are simulated.
32 devices in a mesh: groups: 2 (over y), ep: 16 (over z, x, core).
Axes of the slice: x: 2, y: 2, z: 4, core: 2. Of those that a mesh axis runs over, the one named last changes fastest.
Arguments:
- residual_in: bfloat16 [64, 4096], P(('groups', 'ep')), parts along dimension 0, may hold values from -6 to 6
- queries: bfloat16 [64, 4096], P(('groups', 'ep')), parts along dimension 0, may hold values from -144 to 144
- fresh_keys: bfloat16 [64, 512], P(('groups', 'ep')), parts along dimension 0, may hold values from -6 to 6
- fresh_values: bfloat16 [64, 512], P(('groups', 'ep')), parts along dimension 0, may hold values from -6 to 6
- stored_keys: bfloat16 [64, 256, 512], P(('groups', 'ep')), parts along dimension 0, may hold values from -6 to 6
- stored_values: bfloat16 [64, 256, 512], P(('groups', 'ep')), parts along dimension 0, may hold values from -6 to 6
- context_len: int32 [64], P(('groups', 'ep')), parts along dimension 0, may hold values from 2 to 256
- norm_gain: float32 [4096], replicated, may hold values from 0.5 to 1.5
- expert_ids: int32 [64, 2], P(('groups', 'ep')), parts along dimension 0, may hold values from 0 to 3, all different within a row; in each aligned block of 2 rows (0 to 1, 2 to 3, ...) at most 2 rows name the same one
- expert_gates: bfloat16 [64, 2], P(('groups', 'ep')), parts along dimension 0, may hold values from 0.19921875 to 1
- gate_weight: bfloat16 [4096, 49152], P(None, 'ep'), may hold values from -0.09375 to 0.09375
- up_weight: bfloat16 [4096, 49152], P(None, 'ep'), may hold values from -0.09375 to 0.09375
- down_weight: bfloat16 [49152, 4096], P('ep'), may hold values from -0.0546875 to 0.0546875
Outputs:
- mixed: bfloat16 [64, 4096], P(('groups', 'ep')), parts along dimension 0
There are 2 independent parts, one for each index of `groups`. A program takes and returns all parts, laid end to end along the dimension named above; an argument that names none is the same for every part. Nothing has to cross between parts.
Inputs may be any that keep to these rules, and one draw needn't show every extreme that they name: `expert_ids`: each row names 2 different experts. In the rows of one device no expert is named more than 2 times, and in some device's rows some expert is named exactly 2 times.
All inputs are finite; a program needn't handle non-finite values.
Results may differ from a plain program's by a relative error of at most 0.006.
Values may be sent and summed in bfloat16 or wider, within the bound.
A program may use at most 128 MiB of HBM per device.

v0:
```python
import functools
import math

import jax
import jax.numpy as jnp
from jax import lax
from jax.experimental import pallas as pl
from jax.experimental.pallas import tpu as pltpu
from jax.sharding import PartitionSpec as P

KEY_VALUE_HEADS = 4
HEAD_WIDTH = 128
EXPERTS = 4
CHUNK = 512
RING = 5
EARLY = 3

norm_eps = 1e-05
MESH = pl.DeviceIdType.MESH


def attend(q_ref, fk_ref, fv_ref, k_ref, v_ref, ctx_ref, q_rows, att):
    reqs, features = q_ref.shape
    positions = k_ref.shape[1]
    heads = features // HEAD_WIDTH
    group = heads // KEY_VALUE_HEADS
    scale = 1.0 / math.sqrt(HEAD_WIDTH)
    q = q_ref[...].astype(jnp.float32)
    fk = fk_ref[...].astype(jnp.float32)
    fv = fv_ref[...].astype(jnp.float32)
    for r in range(reqs):
        for h in range(heads):
            q_rows[r * heads + h : r * heads + h + 1, :] = q[
                r : r + 1, h * HEAD_WIDTH : (h + 1) * HEAD_WIDTH
            ]
    scores, own, valid = [], [], []
    position = lax.broadcasted_iota(jnp.int32, (heads, positions), 1)
    for r in range(reqs):
        valid.append(position < ctx_ref[r])
        for j in range(KEY_VALUE_HEADS):
            rows = slice(r * heads + j * group, r * heads + (j + 1) * group)
            cols = slice(j * HEAD_WIDTH, (j + 1) * HEAD_WIDTH)
            qj = q_rows[rows, :]
            scores.append(
                lax.dot_general(
                    qj.astype(jnp.bfloat16),
                    k_ref[r, :, cols],
                    (((1,), (1,)), ((), ())),
                    preferred_element_type=jnp.float32,
                )
            )
            own.append(jnp.sum(qj * fk[r : r + 1, cols], axis=1, keepdims=True))
    ok = jnp.concatenate(valid, axis=0)
    s = jnp.concatenate(scores, axis=0) * scale
    o = jnp.concatenate(own, axis=0) * scale
    m = jnp.maximum(jnp.max(jnp.where(ok, s, -1e30), axis=1, keepdims=True), o)
    e = jnp.where(ok, jnp.exp(s - m), 0.0)
    oe = jnp.exp(o - m)
    total = jnp.sum(e, axis=1, keepdims=True) + oe
    w = (e / total).astype(jnp.bfloat16)
    ow = (oe / total).astype(jnp.bfloat16).astype(jnp.float32)
    for r in range(reqs):
        for j in range(KEY_VALUE_HEADS):
            rows = slice(r * heads + j * group, r * heads + (j + 1) * group)
            cols = slice(j * HEAD_WIDTH, (j + 1) * HEAD_WIDTH)
            mixed = jnp.dot(w[rows], v_ref[r, :, cols], preferred_element_type=jnp.float32)
            mixed = mixed + ow[rows] * fv[r : r + 1, cols]
            for g in range(group):
                h = j * group + g
                att[r : r + 1, h * HEAD_WIDTH : (h + 1) * HEAD_WIDTH] = mixed[g : g + 1, :]


def kernel(
    n,
    *refs,
):
    small_hbm, refs = refs[:10], refs[10:]
    small, refs = refs[4:14], refs[:4] + refs[14:]
    (
    wg_hbm,
    wu_hbm,
    wd_hbm,
    out_ref,
    wg,
    wu,
    wd,
    q_rows,
    residual,
    xr,
    x32,
    acc_g,
    acc_u,
    hidden,
    ys,
    yr,
    in_sem,
    g_sem,
    u_sem,
    d_sem,
    x_send,
    x_recv,
    y_send,
    y_recv,
    ) = refs
    ctx_ref, res_ref, q_ref, fk_ref, fv_ref, gain_ref, ids_ref, gates_ref, k_buf, v_buf = small
    me = lax.axis_index("ep")
    split = n // EXPERTS
    reqs, features = res_ref.shape
    k_steps = features // CHUNK
    ring = wg.shape[0]

    loads = [
        pltpu.make_async_copy(source, target, in_sem.at[i])
        for i, (source, target) in enumerate(zip(small_hbm, small))
    ]
    for load in loads:
        load.start()

    def gate_copy(step, slot):
        rows = pl.ds(pl.multiple_of(step * CHUNK, CHUNK), CHUNK)
        return pltpu.make_async_copy(wg_hbm.at[rows, :], wg.at[slot], g_sem.at[slot])

    def up_copy(step, slot):
        rows = pl.ds(pl.multiple_of(step * CHUNK, CHUNK), CHUNK)
        return pltpu.make_async_copy(wu_hbm.at[rows, :], wu.at[slot], u_sem.at[slot])

    def down_copy(step):
        cols = pl.ds(pl.multiple_of(step * CHUNK, CHUNK), CHUNK)
        return pltpu.make_async_copy(wd_hbm.at[:, cols], wd.at[step], d_sem.at[step])

    early = min(EARLY, k_steps)
    for step in range(ring):
        gate_copy(step, step).start(priority=1)
        up_copy(step, step).start(priority=1)
    for step in range(early):
        down_copy(step).start(priority=1)

    barrier = pltpu.get_barrier_semaphore()

    @pl.loop(1, n)
    def _(d):
        pl.semaphore_signal(
            barrier, inc=1, device_id={"ep": lax.rem(me + d, n)}, device_id_type=MESH
        )

    acc_g[...] = jnp.zeros_like(acc_g)
    acc_u[...] = jnp.zeros_like(acc_u)
    for load in loads:
        load.wait()
    attend(q_ref, fk_ref, fv_ref, k_buf, v_buf, ctx_ref, q_rows, residual)
    full = res_ref[...].astype(jnp.float32) + residual[...]
    residual[...] = full
    factor = lax.rsqrt(jnp.mean(full * full, axis=1, keepdims=True) + norm_eps)
    normed = (full * factor * gain_ref[...]).astype(jnp.bfloat16)
    for k in range(k_steps):
        xr[k, 0] = normed[:, k * CHUNK : (k + 1) * CHUNK]

    pl.semaphore_wait(barrier, n - 1)

    ahead = k_steps

    def send_rows(k):
        @pl.loop(1, n)
        def _(d):
            pltpu.make_async_remote_copy(
                src_ref=xr.at[k, 0],
                dst_ref=xr.at[k, d],
                send_sem=x_send.at[k],
                recv_sem=x_recv.at[k],
                device_id={"ep": lax.rem(me + d, n)},
                device_id_type=MESH,
            ).start()

    for k in range(ahead):
        send_rows(k)

    def wait_blocks(ref, sem):
        pltpu.make_async_copy(ref, ref, sem).wait()

    @pl.loop(0, k_steps)
    def _(k):
        slot = lax.rem(k, ring)

        @pl.when(k + ahead < k_steps)
        def _():
            send_rows(k + ahead)

        wait_blocks(xr.at[k, pl.ds(1, n - 1)], x_recv.at[k])
        for d in range(n):
            x32[reqs * d : reqs * (d + 1), :] = xr[k, d].astype(jnp.float32)
        x = x32[...].astype(jnp.bfloat16)
        gate_copy(k, slot).wait()
        acc_g[...] += jnp.dot(x, wg[slot], preferred_element_type=jnp.float32)
        up_copy(k, slot).wait()
        acc_u[...] += jnp.dot(x, wu[slot], preferred_element_type=jnp.float32)

        @pl.when(k + ring < k_steps)
        def _():
            gate_copy(k + ring, slot).start(priority=1)
            up_copy(k + ring, slot).start(priority=1)

        @pl.when(k == max(k_steps - ring - 1, 0))
        def _():
            @pl.loop(early, k_steps)
            def _(j):
                down_copy(j).start(priority=1)

    gate = acc_g[...]
    hidden[...] = (gate / (1.0 + jnp.exp(-gate)) * acc_u[...]).astype(jnp.bfloat16)

    @pl.loop(0, k_steps)
    def _(j):
        down_copy(j).wait()
        part = jnp.dot(hidden[...], wd[j], preferred_element_type=jnp.float32)
        yr[j, 0] = part[0:reqs].astype(jnp.bfloat16)
        for d in range(1, n):
            ys[j, d] = part[reqs * d : reqs * (d + 1)].astype(jnp.bfloat16)

        @pl.loop(1, n)
        def _(d):
            pltpu.make_async_remote_copy(
                src_ref=ys.at[j, d],
                dst_ref=yr.at[j, d],
                send_sem=y_send.at[j],
                recv_sem=y_recv.at[j],
                device_id={"ep": lax.rem(me - d + n, n)},
                device_id_type=MESH,
            ).start()

    ids = ids_ref[...]
    gates = gates_ref[...].astype(jnp.float32)
    weights = []
    for expert in range(EXPERTS):
        weights.append(jnp.sum(jnp.where(ids == expert, gates, 0.0), axis=1, keepdims=True))

    for j in range(k_steps):
        cols = slice(j * CHUNK, (j + 1) * CHUNK)
        wait_blocks(yr.at[j, pl.ds(1, n - 1)], y_recv.at[j])
        total = residual[:, cols]
        for d in range(n):
            expert = lax.rem(me + d, n) // split
            weight = weights[0]
            for other in range(1, EXPERTS):
                weight = jnp.where(expert == other, weights[other], weight)
            total = total + weight * yr[j, d].astype(jnp.float32)
        out_ref[:, cols] = total.astype(out_ref.dtype)

    @pl.loop(0, k_steps)
    def _(k):
        wait_blocks(xr.at[k, pl.ds(1, n - 1)], x_send.at[k])
        wait_blocks(ys.at[k, pl.ds(1, n - 1)], y_send.at[k])


def local(
    residual_in,
    queries,
    fresh_keys,
    fresh_values,
    stored_keys,
    stored_values,
    context_len,
    norm_gain,
    expert_ids,
    expert_gates,
    gate_weight,
    up_weight,
    down_weight,
):
    n = lax.axis_size("ep")
    reqs, features = residual_in.shape
    units = gate_weight.shape[1]
    steps = features // CHUNK
    ring = min(RING, steps)
    bf16, f32 = jnp.bfloat16, jnp.float32
    vmem = pl.BlockSpec(memory_space=pltpu.VMEM)
    hbm = pl.BlockSpec(memory_space=pl.ANY)
    dma = pltpu.SemaphoreType.DMA
    rows = n * reqs
    return pl.pallas_call(
        functools.partial(kernel, n),
        out_shape=jax.ShapeDtypeStruct((reqs, features), bf16),
        in_specs=[hbm] * 13,
        out_specs=vmem,
        scratch_shapes=[
            pltpu.SMEM(context_len.shape, jnp.int32),
            pltpu.VMEM((reqs, features), bf16),
            pltpu.VMEM((reqs, features), bf16),
            pltpu.VMEM(fresh_keys.shape, bf16),
            pltpu.VMEM(fresh_values.shape, bf16),
            pltpu.VMEM((1, features), f32),
            pltpu.VMEM(expert_ids.shape, jnp.int32),
            pltpu.VMEM(expert_gates.shape, bf16),
            pltpu.VMEM(stored_keys.shape, bf16),
            pltpu.VMEM(stored_values.shape, bf16),
            pltpu.VMEM((ring, CHUNK, units), bf16),
            pltpu.VMEM((ring, CHUNK, units), bf16),
            pltpu.VMEM((steps, units, CHUNK), bf16),
            pltpu.VMEM((reqs * features // HEAD_WIDTH, HEAD_WIDTH), f32),
            pltpu.VMEM((reqs, features), f32),
            pltpu.VMEM((steps, n, reqs, CHUNK), bf16),
            pltpu.VMEM((rows, CHUNK), f32),
            pltpu.VMEM((rows, units), f32),
            pltpu.VMEM((rows, units), f32),
            pltpu.VMEM((rows, units), bf16),
            pltpu.VMEM((steps, n, reqs, CHUNK), bf16),
            pltpu.VMEM((steps, n, reqs, CHUNK), bf16),
            dma((10,)),
            dma((ring,)),
            dma((ring,)),
            dma((steps,)),
            dma((steps,)),
            dma((steps,)),
            dma((steps,)),
            dma((steps,)),
        ],
        compiler_params=pltpu.CompilerParams(
            collective_id=0, has_side_effects=True, vmem_limit_bytes=66_000_000
        ),
        name="decode_step",
    )(
        context_len,
        residual_in,
        queries,
        fresh_keys,
        fresh_values,
        norm_gain.reshape(1, features),
        expert_ids,
        expert_gates,
        stored_keys,
        stored_values,
        gate_weight,
        up_weight,
        down_weight,
    )


def solution(mesh):
    in_specs = (
        P(("groups", "ep"), None),
        P(("groups", "ep"), None),
        P(("groups", "ep"), None),
        P(("groups", "ep"), None),
        P(("groups", "ep"), None, None),
        P(("groups", "ep"), None, None),
        P(("groups", "ep")),
        P(),
        P(("groups", "ep"), None),
        P(("groups", "ep"), None),
        P(None, "ep"),
        P(None, "ep"),
        P("ep", None),
    )
    out_specs = P(("groups", "ep"), None)
    return jax.shard_map(local, mesh=mesh, in_specs=in_specs, out_specs=out_specs, check_vma=False)
```

profile of v0, /device:TPU:0, one launch (start us, length us, event | category | flops | bytes accessed | tf_op | source)
XLA Modules:
  0.0 36.6 jit_solution(5765269494683156687)
XLA Ops:
  0.0 35.2 %decode_step.1 = bf16[2,4096]{1,0:T(2,128)(2,1)} custom-call(s32[2]{0:T(128)} %refs_0_.1, bf16[2,4096]{1,0:T(2,128)(2,1)} %refs_1_.1, bf16[2,4096]{1,0:T(2,128)(2,1)} %refs_2_.1, bf16[2,512]{1,0:T(2,128)(2,1)} %refs_3_.1, bf16[2,512]{1,0:T(2,128)(2,1)} %refs_4_.1, f32[1,4096]{1,0:T(1,128)} %bitcast.1, s32[2,2]{1,0:T(2,128)} %refs_6_.1, ...), custom_call_target="tpu_custom_call" | custom-call | tf_op jit(solution)/shard_map/decode_step/pallas_call | solution.py:279
  35.2 1.3 %copy.15 = bf16[2,4096]{1,0:T(2,128)(2,1)} copy(bf16[2,4096]{1,0:T(2,128)(2,1)} %decode_step.1) | data formatting | bytes 32768
where the time goes:
time: 36.8 us; the launch traced here: 36.6 us
  Pallas kernels  35.2 us (96%)
  local copies, waits for them, and re-layouts  1.34 us (4%)
    pallas_call x1, Pallas kernels, local(): pl.pallas_call(functools.partial(kernel, n), out_shape=jax.ShapeDtypeStru...  35.2 us
    unnamed x1, local copies, waits for them, and re-layouts  1.34 us

commit v1 on v0

--- a/solution.py
+++ b/solution.py
@@ -14,6 +14,9 @@
 CHUNK = 512
 RING = 5
 EARLY = 3
+IN_CHUNK = 512
+OUT_CHUNK = 512
+LAG = 2
 
 norm_eps = 1e-05
 MESH = pl.DeviceIdType.MESH
@@ -70,6 +73,329 @@
                 att[r : r + 1, h * HEAD_WIDTH : (h + 1) * HEAD_WIDTH] = mixed[g : g + 1, :]
 
 
+def shared_kernel(groups, n, *refs):
+    small_hbm, refs = refs[:10], refs[10:]
+    small, refs = refs[4:14], refs[:4] + refs[14:]
+    (
+        wg_hbm,
+        wu_hbm,
+        wd_hbm,
+        out_ref,
+        wg,
+        wu,
+        wd,
+        q_rows,
+        residual,
+        xs,
+        xd,
+        xf,
+        x32,
+        acc_g,
+        acc_u,
+        hidden,
+        keep,
+        ps,
+        pr,
+        ys,
+        yr,
+        in_sem,
+        g_sem,
+        u_sem,
+        d_sem,
+        x_send,
+        x_recv,
+        f_send,
+        f_recv,
+        p_send,
+        p_recv,
+        y_send,
+        y_recv,
+    ) = refs
+    ctx_ref, res_ref, q_ref, fk_ref, fv_ref, gain_ref, ids_ref, gates_ref, k_buf, v_buf = small
+    g, e = lax.axis_index("groups"), lax.axis_index("ep")
+    per_group = n // 2
+    chips = groups * per_group
+    core = lax.rem(e, 2)
+    chip = g * per_group + e // 2
+    partner = {"groups": g, "ep": e + 1 - 2 * core}
+    reqs, features = res_ref.shape
+    k_steps, chunk, units = wg.shape
+    j_steps, _, out_chunk = wd.shape
+    rows = chips * reqs
+
+    def across(d):
+        q = lax.rem(chip + d, chips)
+        return {"groups": q // per_group, "ep": lax.rem(q, per_group) * 2 + 1 - core}
+
+    loads = [
+        pltpu.make_async_copy(source, target, in_sem.at[i])
+        for i, (source, target) in enumerate(zip(small_hbm, small))
+    ]
+    for load in loads:
+        load.start()
+
+    first = pl.multiple_of(g * units, 128)
+
+    def gate_copy(step):
+        at = pl.ds(pl.multiple_of(step * chunk, chunk), chunk)
+        return pltpu.make_async_copy(wg_hbm.at[at, pl.ds(first, units)], wg.at[step], g_sem.at[step])
+
+    def up_copy(step):
+        at = pl.ds(pl.multiple_of(step * chunk, chunk), chunk)
+        return pltpu.make_async_copy(wu_hbm.at[at, pl.ds(first, units)], wu.at[step], u_sem.at[step])
+
+    def down_copy(step):
+        at = pl.ds(pl.multiple_of(step * out_chunk, out_chunk), out_chunk)
+        return pltpu.make_async_copy(wd_hbm.at[pl.ds(first, units), at], wd.at[step], d_sem.at[step])
+
+    @pl.loop(0, k_steps)
+    def _(step):
+        gate_copy(step).start(priority=1)
+        up_copy(step).start(priority=1)
+
+    @pl.loop(0, j_steps)
+    def _(step):
+        down_copy(step).start(priority=1)
+
+    barrier = pltpu.get_barrier_semaphore()
+
+    @pl.loop(0, chips)
+    def _(d):
+        pl.semaphore_signal(barrier, inc=1, device_id=across(d), device_id_type=MESH)
+
+    acc_g[...] = jnp.zeros_like(acc_g)
+    acc_u[...] = jnp.zeros_like(acc_u)
+    for load in loads:
+        load.wait()
+    attend(q_ref, fk_ref, fv_ref, k_buf, v_buf, ctx_ref, q_rows, residual)
+    full = res_ref[...].astype(jnp.float32) + residual[...]
+    residual[...] = full
+    factor = lax.rsqrt(jnp.mean(full * full, axis=1, keepdims=True) + norm_eps)
+    normed = (full * factor * gain_ref[...]).astype(jnp.bfloat16)
+    for k in range(k_steps):
+        xs[k] = normed[:, k * chunk : (k + 1) * chunk]
+
+    pl.semaphore_wait(barrier, chips)
+
+    @pl.loop(0, k_steps)
+    def _(k):
+        @pl.loop(0, chips)
+        def _(d):
+            pltpu.make_async_remote_copy(
+                src_ref=xs.at[k],
+                dst_ref=xd.at[k, chip],
+                send_sem=x_send.at[k],
+                recv_sem=x_recv.at[k],
+                device_id=across(d),
+                device_id_type=MESH,
+            ).start()
+
+    def wait_for(ref, sem):
+        pltpu.make_async_copy(ref, ref, sem).wait()
+
+    def forward(k):
+        return pltpu.make_async_remote_copy(
+            src_ref=xd.at[k],
+            dst_ref=xf.at[k],
+            send_sem=f_send.at[k],
+            recv_sem=f_recv.at[k],
+            device_id=partner,
+            device_id_type=MESH,
+        )
+
+    def pass_on(k):
+        wait_for(xd.at[k], x_recv.at[k])
+        forward(k).start()
+
+    pass_on(0)
+
+    @pl.loop(0, k_steps)
+    def _(k):
+        @pl.when(k + 1 < k_steps)
+        def _():
+            pass_on(k + 1)
+
+        forward(k).wait_recv()
+        for q in range(chips):
+            x32[reqs * q : reqs * (q + 1), :] = xd[k, q].astype(jnp.float32)
+            x32[rows + reqs * q : rows + reqs * (q + 1), :] = xf[k, q].astype(jnp.float32)
+        x = x32[...].astype(jnp.bfloat16)
+        gate_copy(k).wait()
+        acc_g[...] += jnp.dot(x, wg[k], preferred_element_type=jnp.float32)
+        up_copy(k).wait()
+        acc_u[...] += jnp.dot(x, wu[k], preferred_element_type=jnp.float32)
+
+    gate = acc_g[...]
+    hidden[...] = (gate / (1.0 + jnp.exp(-gate)) * acc_u[...]).astype(jnp.bfloat16)
+
+    def give(j):
+        return pltpu.make_async_remote_copy(
+            src_ref=ps.at[j],
+            dst_ref=pr.at[j],
+            send_sem=p_send.at[j],
+            recv_sem=p_recv.at[j],
+            device_id=partner,
+            device_id_type=MESH,
+        )
+
+    def send_back(j):
+        give(j).wait_recv()
+        both = (keep[j] + pr[j].astype(jnp.float32)).astype(jnp.bfloat16)
+        for q in range(chips):
+            ys[j, q] = both[reqs * q : reqs * (q + 1)]
+
+        @pl.loop(0, chips)
+        def _(d):
+            pltpu.make_async_remote_copy(
+                src_ref=ys.at[j, lax.rem(chip + d, chips)],
+                dst_ref=yr.at[j, chip],
+                send_sem=y_send.at[j],
+                recv_sem=y_recv.at[j],
+                device_id=across(d),
+                device_id_type=MESH,
+            ).start()
+
+    lag = min(LAG, j_steps)
+
+    @pl.loop(0, j_steps)
+    def _(j):
+        down_copy(j).wait()
+        part = jnp.dot(hidden[...], wd[j], preferred_element_type=jnp.float32)
+        keep[j] = part[0:rows]
+        ps[j] = part[rows:].astype(jnp.bfloat16)
+        give(j).start()
+
+        @pl.when(j >= lag)
+        def _():
+            send_back(j - lag)
+
+    @pl.loop(j_steps - lag, j_steps)
+    def _(j):
+        send_back(j)
+
+    ids = ids_ref[...]
+    gates = gates_ref[...].astype(jnp.float32)
+    per_expert = per_group // EXPERTS
+    weights = []
+    for expert in range(EXPERTS):
+        weights.append(jnp.sum(jnp.where(ids == expert, gates, 0.0), axis=1, keepdims=True))
+
+    for j in range(j_steps):
+        cols = slice(j * out_chunk, (j + 1) * out_chunk)
+        wait_for(yr.at[j], y_recv.at[j])
+        total = residual[:, cols]
+        for expert in range(EXPERTS):
+            share = None
+            for group in range(groups):
+                for i in range(per_expert):
+                    term = yr[j, group * per_group + expert * per_expert + i].astype(jnp.float32)
+                    share = term if share is None else share + term
+            total = total + weights[expert] * share
+        out_ref[:, cols] = total.astype(out_ref.dtype)
+
+    @pl.loop(0, k_steps)
+    def _(k):
+        wait_for(xd.at[k], x_send.at[k])
+        forward(k).wait_send()
+
+    @pl.loop(0, j_steps)
+    def _(j):
+        give(j).wait_send()
+        wait_for(ys.at[j], y_send.at[j])
+
+
+def shared_local(
+    residual_in,
+    queries,
+    fresh_keys,
+    fresh_values,
+    stored_keys,
+    stored_values,
+    context_len,
+    norm_gain,
+    expert_ids,
+    expert_gates,
+    gate_weight,
+    up_weight,
+    down_weight,
+):
+    groups, n = lax.axis_size("groups"), lax.axis_size("ep")
+    reqs, features = residual_in.shape
+    units = gate_weight.shape[1] // groups
+    chips = groups * n // 2
+    rows = chips * reqs
+    k_steps, j_steps = features // IN_CHUNK, features // OUT_CHUNK
+    bf16, f32 = jnp.bfloat16, jnp.float32
+    vmem = pl.BlockSpec(memory_space=pltpu.VMEM)
+    hbm = pl.BlockSpec(memory_space=pl.ANY)
+    dma = pltpu.SemaphoreType.DMA
+    return pl.pallas_call(
+        functools.partial(shared_kernel, groups, n),
+        out_shape=jax.ShapeDtypeStruct((reqs, features), bf16),
+        in_specs=[hbm] * 13,
+        out_specs=vmem,
+        scratch_shapes=[
+            pltpu.SMEM(context_len.shape, jnp.int32),
+            pltpu.VMEM((reqs, features), bf16),
+            pltpu.VMEM((reqs, features), bf16),
+            pltpu.VMEM(fresh_keys.shape, bf16),
+            pltpu.VMEM(fresh_values.shape, bf16),
+            pltpu.VMEM((1, features), f32),
+            pltpu.VMEM(expert_ids.shape, jnp.int32),
+            pltpu.VMEM(expert_gates.shape, bf16),
+            pltpu.VMEM(stored_keys.shape, bf16),
+            pltpu.VMEM(stored_values.shape, bf16),
+            pltpu.VMEM((k_steps, IN_CHUNK, units), bf16),
+            pltpu.VMEM((k_steps, IN_CHUNK, units), bf16),
+            pltpu.VMEM((j_steps, units, OUT_CHUNK), bf16),
+            pltpu.VMEM((reqs * features // HEAD_WIDTH, HEAD_WIDTH), f32),
+            pltpu.VMEM((reqs, features), f32),
+            pltpu.VMEM((k_steps, reqs, IN_CHUNK), bf16),
+            pltpu.VMEM((k_steps, chips, reqs, IN_CHUNK), bf16),
+            pltpu.VMEM((k_steps, chips, reqs, IN_CHUNK), bf16),
+            pltpu.VMEM((2 * rows, IN_CHUNK), f32),
+            pltpu.VMEM((2 * rows, units), f32),
+            pltpu.VMEM((2 * rows, units), f32),
+            pltpu.VMEM((2 * rows, units), bf16),
+            pltpu.VMEM((j_steps, rows, OUT_CHUNK), f32),
+            pltpu.VMEM((j_steps, rows, OUT_CHUNK), bf16),
+            pltpu.VMEM((j_steps, rows, OUT_CHUNK), bf16),
+            pltpu.VMEM((j_steps, chips, reqs, OUT_CHUNK), bf16),
+            pltpu.VMEM((j_steps, chips, reqs, OUT_CHUNK), bf16),
+            dma((10,)),
+            dma((k_steps,)),
+            dma((k_steps,)),
+            dma((j_steps,)),
+            dma((k_steps,)),
+            dma((k_steps,)),
+            dma((k_steps,)),
+            dma((k_steps,)),
+            dma((j_steps,)),
+            dma((j_steps,)),
+            dma((j_steps,)),
+            dma((j_steps,)),
+        ],
+        compiler_params=pltpu.CompilerParams(
+            collective_id=0, has_side_effects=True, vmem_limit_bytes=66_000_000
+        ),
+        name="decode_step",
+    )(
+        context_len,
+        residual_in,
+        queries,
+        fresh_keys,
+        fresh_values,
+        norm_gain.reshape(1, features),
+        expert_ids,
+        expert_gates,
+        stored_keys,
+        stored_values,
+        gate_weight,
+        up_weight,
+        down_weight,
+    )
+
+
 def kernel(
     n,
     *refs,
@@ -251,7 +577,7 @@
         wait_blocks(ys.at[k, pl.ds(1, n - 1)], y_send.at[k])
 
 
-def local(
+def plain_local(
     residual_in,
     queries,
     fresh_keys,
@@ -351,4 +677,11 @@
         P("ep", None),
     )
     out_specs = P(("groups", "ep"), None)
+    groups, n = mesh.shape["groups"], mesh.shape["ep"]
+
+    def local(*args):
+        units = args[10].shape[1]
+        shared = n % (2 * EXPERTS) == 0 and units % (128 * groups) == 0
+        return (shared_local if shared else plain_local)(*args)
+
     return jax.shard_map(local, mesh=mesh, in_specs=in_specs, out_specs=out_specs, check_vma=False)

time: 36.8 us -> 32.5 us (0.88)
  Pallas kernels: 35.2 us -> 30.9 us
    pallas_call x1, Pallas kernels: 35.2 us -> 30.9 us  [shared_local(): pl.pallas_call(functools.partial(shared_kernel, groups, n), out_shape=jax...]
where the time goes in v1:
time: 32.5 us; the launch traced here: 32.3 us
  Pallas kernels  30.9 us (95%)
  local copies, waits for them, and re-layouts  1.34 us (4%)
    pallas_call x1, Pallas kernels, shared_local(): pl.pallas_call(functools.partial(shared_kernel, groups, n), out_shape=jax...  30.9 us
    unnamed x1, local copies, waits for them, and re-layouts  1.34 us

profile of v1, /device:TPU:0, one launch (start us, length us, event | category | flops | bytes accessed | tf_op | source)
XLA Modules:
  0.0 32.3 jit_solution(14771723034619446994)
XLA Ops:
  0.0 30.9 %decode_step.1 = bf16[2,4096]{1,0:T(2,128)(2,1)} custom-call(s32[2]{0:T(128)} %refs_0_.1, bf16[2,4096]{1,0:T(2,128)(2,1)} %refs_1_.1, bf16[2,4096]{1,0:T(2,128)(2,1)} %refs_2_.1, bf16[2,512]{1,0:T(2,128)(2,1)} %refs_3_.1, bf16[2,512]{1,0:T(2,128)(2,1)} %refs_4_.1, f32[1,4096]{1,0:T(1,128)} %bitcast.1, s32[2,2]{1,0:T(2,128)} %refs_6_.1, ...), custom_call_target="tpu_custom_call" | custom-call | tf_op jit(solution)/shard_map/decode_step/pallas_call | solution.py:332
  30.9 1.3 %copy.15 = bf16[2,4096]{1,0:T(2,128)(2,1)} copy(bf16[2,4096]{1,0:T(2,128)(2,1)} %decode_step.1) | data formatting | bytes 32768

commit v2 on v1

--- a/solution.py
+++ b/solution.py
@@ -14,9 +14,10 @@
 CHUNK = 512
 RING = 5
 EARLY = 3
-IN_CHUNK = 512
-OUT_CHUNK = 512
-LAG = 2
+IN_CHUNK = 1024
+OUT_CHUNK = 1024
+LAG = 1
+SHARED_VMEM = 66_000_000
 
 norm_eps = 1e-05
 MESH = pl.DeviceIdType.MESH
@@ -89,7 +90,7 @@
         xs,
         xd,
         xf,
-        x32,
+        x32s,
         acc_g,
         acc_u,
         hidden,
@@ -99,9 +100,7 @@
         ys,
         yr,
         in_sem,
-        g_sem,
-        u_sem,
-        d_sem,
+        w_sem,
         x_send,
         x_recv,
         f_send,
@@ -123,9 +122,27 @@
     j_steps, _, out_chunk = wd.shape
     rows = chips * reqs
 
-    def across(d):
-        q = lax.rem(chip + d, chips)
-        return {"groups": q // per_group, "ep": lax.rem(q, per_group) * 2 + 1 - core}
+    place = e // 2
+
+    def turned(at, by, size):
+        moved = at + by
+        return moved - jnp.where(moved >= size, size, 0)
+
+    targets = []
+    near = sorted(range(per_group), key=lambda t: abs(t - per_group // 2))
+    for t in near:
+        for s in reversed(range(groups)):
+            to_group, to_place = turned(g, s, groups), turned(place, t, per_group)
+            targets.append(
+                (
+                    to_group * per_group + to_place,
+                    {"groups": to_group, "ep": to_place * 2 + 1 - core},
+                )
+            )
+
+    barrier = pltpu.get_barrier_semaphore()
+    for _, device in targets:
+        pl.semaphore_signal(barrier, inc=1, device_id=device, device_id_type=MESH)
 
     loads = [
         pltpu.make_async_copy(source, target, in_sem.at[i])
@@ -138,15 +155,15 @@
 
     def gate_copy(step):
         at = pl.ds(pl.multiple_of(step * chunk, chunk), chunk)
-        return pltpu.make_async_copy(wg_hbm.at[at, pl.ds(first, units)], wg.at[step], g_sem.at[step])
+        return pltpu.make_async_copy(wg_hbm.at[at, pl.ds(first, units)], wg.at[step], w_sem.at[0])
 
     def up_copy(step):
         at = pl.ds(pl.multiple_of(step * chunk, chunk), chunk)
-        return pltpu.make_async_copy(wu_hbm.at[at, pl.ds(first, units)], wu.at[step], u_sem.at[step])
+        return pltpu.make_async_copy(wu_hbm.at[at, pl.ds(first, units)], wu.at[step], w_sem.at[1])
 
     def down_copy(step):
         at = pl.ds(pl.multiple_of(step * out_chunk, out_chunk), out_chunk)
-        return pltpu.make_async_copy(wd_hbm.at[pl.ds(first, units), at], wd.at[step], d_sem.at[step])
+        return pltpu.make_async_copy(wd_hbm.at[pl.ds(first, units), at], wd.at[step], w_sem.at[2])
 
     @pl.loop(0, k_steps)
     def _(step):
@@ -156,12 +173,6 @@
     @pl.loop(0, j_steps)
     def _(step):
         down_copy(step).start(priority=1)
-
-    barrier = pltpu.get_barrier_semaphore()
-
-    @pl.loop(0, chips)
-    def _(d):
-        pl.semaphore_signal(barrier, inc=1, device_id=across(d), device_id_type=MESH)
 
     acc_g[...] = jnp.zeros_like(acc_g)
     acc_u[...] = jnp.zeros_like(acc_u)
@@ -179,14 +190,13 @@
 
     @pl.loop(0, k_steps)
     def _(k):
-        @pl.loop(0, chips)
-        def _(d):
+        for _, device in targets:
             pltpu.make_async_remote_copy(
                 src_ref=xs.at[k],
                 dst_ref=xd.at[k, chip],
-                send_sem=x_send.at[k],
+                send_sem=x_send.at[0],
                 recv_sem=x_recv.at[k],
-                device_id=across(d),
+                device_id=device,
                 device_id_type=MESH,
             ).start()
 
@@ -197,7 +207,7 @@
         return pltpu.make_async_remote_copy(
             src_ref=xd.at[k],
             dst_ref=xf.at[k],
-            send_sem=f_send.at[k],
+            send_sem=f_send.at[0],
             recv_sem=f_recv.at[k],
             device_id=partner,
             device_id_type=MESH,
@@ -208,21 +218,19 @@
         forward(k).start()
 
     pass_on(0)
-
-    @pl.loop(0, k_steps)
-    def _(k):
-        @pl.when(k + 1 < k_steps)
-        def _():
+    for k in range(k_steps):
+        if k + 1 < k_steps:
             pass_on(k + 1)
-
         forward(k).wait_recv()
+        x32 = x32s.at[k % 2]
         for q in range(chips):
             x32[reqs * q : reqs * (q + 1), :] = xd[k, q].astype(jnp.float32)
             x32[rows + reqs * q : rows + reqs * (q + 1), :] = xf[k, q].astype(jnp.float32)
         x = x32[...].astype(jnp.bfloat16)
-        gate_copy(k).wait()
+        if k == 0:
+            wait_for(wg, w_sem.at[0])
+            wait_for(wu, w_sem.at[1])
         acc_g[...] += jnp.dot(x, wg[k], preferred_element_type=jnp.float32)
-        up_copy(k).wait()
         acc_u[...] += jnp.dot(x, wu[k], preferred_element_type=jnp.float32)
 
     gate = acc_g[...]
@@ -232,7 +240,7 @@
         return pltpu.make_async_remote_copy(
             src_ref=ps.at[j],
             dst_ref=pr.at[j],
-            send_sem=p_send.at[j],
+            send_sem=p_send.at[0],
             recv_sem=p_recv.at[j],
             device_id=partner,
             device_id_type=MESH,
@@ -244,34 +252,25 @@
         for q in range(chips):
             ys[j, q] = both[reqs * q : reqs * (q + 1)]
 
-        @pl.loop(0, chips)
-        def _(d):
+        for q, device in targets:
             pltpu.make_async_remote_copy(
-                src_ref=ys.at[j, lax.rem(chip + d, chips)],
+                src_ref=ys.at[j, q],
                 dst_ref=yr.at[j, chip],
-                send_sem=y_send.at[j],
+                send_sem=y_send.at[0],
                 recv_sem=y_recv.at[j],
-                device_id=across(d),
+                device_id=device,
                 device_id_type=MESH,
             ).start()
 
-    lag = min(LAG, j_steps)
-
-    @pl.loop(0, j_steps)
-    def _(j):
-        down_copy(j).wait()
-        part = jnp.dot(hidden[...], wd[j], preferred_element_type=jnp.float32)
-        keep[j] = part[0:rows]
-        ps[j] = part[rows:].astype(jnp.bfloat16)
-        give(j).start()
-
-        @pl.when(j >= lag)
-        def _():
-            send_back(j - lag)
-
-    @pl.loop(j_steps - lag, j_steps)
-    def _(j):
-        send_back(j)
+    wait_for(wd, w_sem.at[2])
+    for j in range(j_steps + LAG):
+        if j < j_steps:
+            part = jnp.dot(hidden[...], wd[j], preferred_element_type=jnp.float32)
+            keep[j] = part[0:rows]
+            ps[j] = part[rows:].astype(jnp.bfloat16)
+            give(j).start()
+        if j >= LAG:
+            send_back(j - LAG)
 
     ids = ids_ref[...]
     gates = gates_ref[...].astype(jnp.float32)
@@ -293,15 +292,10 @@
             total = total + weights[expert] * share
         out_ref[:, cols] = total.astype(out_ref.dtype)
 
-    @pl.loop(0, k_steps)
-    def _(k):
-        wait_for(xd.at[k], x_send.at[k])
-        forward(k).wait_send()
-
-    @pl.loop(0, j_steps)
-    def _(j):
-        give(j).wait_send()
-        wait_for(ys.at[j], y_send.at[j])
+    wait_for(xd, x_send.at[0])
+    wait_for(xd, f_send.at[0])
+    wait_for(ps, p_send.at[0])
+    wait_for(ys, y_send.at[0])
 
 
 def shared_local(
@@ -327,7 +321,7 @@
     k_steps, j_steps = features // IN_CHUNK, features // OUT_CHUNK
     bf16, f32 = jnp.bfloat16, jnp.float32
     vmem = pl.BlockSpec(memory_space=pltpu.VMEM)
-    hbm = pl.BlockSpec(memory_space=pl.ANY)
+    hbm = pl.BlockSpec(memory_space=pltpu.HBM)
     dma = pltpu.SemaphoreType.DMA
     return pl.pallas_call(
         functools.partial(shared_kernel, groups, n),
@@ -353,7 +347,7 @@
             pltpu.VMEM((k_steps, reqs, IN_CHUNK), bf16),
             pltpu.VMEM((k_steps, chips, reqs, IN_CHUNK), bf16),
             pltpu.VMEM((k_steps, chips, reqs, IN_CHUNK), bf16),
-            pltpu.VMEM((2 * rows, IN_CHUNK), f32),
+            pltpu.VMEM((2, 2 * rows, IN_CHUNK), f32),
             pltpu.VMEM((2 * rows, units), f32),
             pltpu.VMEM((2 * rows, units), f32),
             pltpu.VMEM((2 * rows, units), bf16),
@@ -363,20 +357,18 @@
             pltpu.VMEM((j_steps, chips, reqs, OUT_CHUNK), bf16),
             pltpu.VMEM((j_steps, chips, reqs, OUT_CHUNK), bf16),
             dma((10,)),
+            dma((3,)),
+            dma((1,)),
             dma((k_steps,)),
+            dma((1,)),
             dma((k_steps,)),
+            dma((1,)),
             dma((j_steps,)),
-            dma((k_steps,)),
-            dma((k_steps,)),
-            dma((k_steps,)),
-            dma((k_steps,)),
-            dma((j_steps,)),
-            dma((j_steps,)),
-            dma((j_steps,)),
+            dma((1,)),
             dma((j_steps,)),
         ],
         compiler_params=pltpu.CompilerParams(
-            collective_id=0, has_side_effects=True, vmem_limit_bytes=66_000_000
+            collective_id=0, has_side_effects=True, vmem_limit_bytes=SHARED_VMEM
         ),
         name="decode_step",
     )(

time: 32.5 us -> 29.5 us (0.908)
  Pallas kernels: 30.9 us -> 27.9 us
    pallas_call x1, Pallas kernels: 30.9 us -> 27.9 us  [shared_local(): pl.pallas_call(functools.partial(shared_kernel, groups, n), out_shape=jax...]
where the time goes in v2:
time: 29.5 us; the launch traced here: 29.2 us
  Pallas kernels  27.9 us (95%)
  local copies, waits for them, and re-layouts  1.34 us (5%)
    pallas_call x1, Pallas kernels, shared_local(): pl.pallas_call(functools.partial(shared_kernel, groups, n), out_shape=jax...  27.9 us
    unnamed x1, local copies, waits for them, and re-layouts  1.34 us

profile of v2, /device:TPU:0, one launch (start us, length us, event | category | flops | bytes accessed | tf_op | source)
XLA Modules:
  0.0 29.2 jit_solution(9045788703445466499)
XLA Ops:
  0.0 27.9 %decode_step.1 = bf16[2,4096]{1,0:T(2,128)(2,1)} custom-call(s32[2]{0:T(128)} %refs_0_.1, bf16[2,4096]{1,0:T(2,128)(2,1)} %refs_1_.1, bf16[2,4096]{1,0:T(2,128)(2,1)} %refs_2_.1, bf16[2,512]{1,0:T(2,128)(2,1)} %refs_3_.1, bf16[2,512]{1,0:T(2,128)(2,1)} %refs_4_.1, f32[1,4096]{1,0:T(1,128)} %bitcast.1, s32[2,2]{1,0:T(2,128)} %refs_6_.1, ...), custom_call_target="tpu_custom_call" | custom-call | tf_op jit(solution)/shard_map/decode_step/pallas_call | solution.py:326
  27.9 1.3 %copy.15 = bf16[2,4096]{1,0:T(2,128)(2,1)} copy(bf16[2,4096]{1,0:T(2,128)(2,1)} %decode_step.1) | data formatting | bytes 32768

commit v3 on v2

--- a/solution.py
+++ b/solution.py
@@ -14,10 +14,10 @@
 CHUNK = 512
 RING = 5
 EARLY = 3
-IN_CHUNK = 1024
-OUT_CHUNK = 1024
+IN_SPLIT = (2, 2, 2, 2)
+OUT_SPLIT = (1, 2, 2, 3)
 LAG = 1
-SHARED_VMEM = 66_000_000
+LOADS = 4
 
 norm_eps = 1e-05
 MESH = pl.DeviceIdType.MESH
@@ -74,31 +74,22 @@
                 att[r : r + 1, h * HEAD_WIDTH : (h + 1) * HEAD_WIDTH] = mixed[g : g + 1, :]
 
 
+def cut(total, split):
+    unit = total // sum(split)
+    sizes = [unit * part for part in split]
+    return [(sum(sizes[:i]), size) for i, size in enumerate(sizes)]
+
+
 def shared_kernel(groups, n, *refs):
     small_hbm, refs = refs[:10], refs[10:]
     small, refs = refs[4:14], refs[:4] + refs[14:]
+    wg_hbm, wu_hbm, wd_hbm, out_ref, w, wd, q_rows, residual, acc, hidden = refs[:10]
+    refs = refs[10:]
+    ins, outs = len(IN_SPLIT), len(OUT_SPLIT)
+    xs, xd, xf, x32s = (refs[ins * i : ins * (i + 1)] for i in range(4))
+    refs = refs[4 * ins :]
+    keep, ps, pr, ys, yr = (refs[outs * i : outs * (i + 1)] for i in range(5))
     (
-        wg_hbm,
-        wu_hbm,
-        wd_hbm,
-        out_ref,
-        wg,
-        wu,
-        wd,
-        q_rows,
-        residual,
-        xs,
-        xd,
-        xf,
-        x32s,
-        acc_g,
-        acc_u,
-        hidden,
-        keep,
-        ps,
-        pr,
-        ys,
-        yr,
         in_sem,
         w_sem,
         x_send,
@@ -109,7 +100,7 @@
         p_recv,
         y_send,
         y_recv,
-    ) = refs
+    ) = refs[5 * outs :]
     ctx_ref, res_ref, q_ref, fk_ref, fv_ref, gain_ref, ids_ref, gates_ref, k_buf, v_buf = small
     g, e = lax.axis_index("groups"), lax.axis_index("ep")
     per_group = n // 2
@@ -118,8 +109,8 @@
     chip = g * per_group + e // 2
     partner = {"groups": g, "ep": e + 1 - 2 * core}
     reqs, features = res_ref.shape
-    k_steps, chunk, units = wg.shape
-    j_steps, _, out_chunk = wd.shape
+    units = wd.shape[0]
+    in_parts, out_parts = cut(features, IN_SPLIT), cut(features, OUT_SPLIT)
     rows = chips * reqs
 
     place = e // 2
@@ -140,6 +131,10 @@
                 )
             )
 
+    owners = []
+    for q in sorted(range(chips), key=lambda q: (q // per_group) + (q % per_group)):
+        owners.append((q, {"groups": q // per_group, "ep": (q % per_group) * 2 + 1 - core}))
+
     barrier = pltpu.get_barrier_semaphore()
     for _, device in targets:
         pl.semaphore_signal(barrier, inc=1, device_id=device, device_id_type=MESH)
@@ -153,29 +148,23 @@
 
     first = pl.multiple_of(g * units, 128)
 
-    def gate_copy(step):
-        at = pl.ds(pl.multiple_of(step * chunk, chunk), chunk)
-        return pltpu.make_async_copy(wg_hbm.at[at, pl.ds(first, units)], wg.at[step], w_sem.at[0])
-
-    def up_copy(step):
-        at = pl.ds(pl.multiple_of(step * chunk, chunk), chunk)
-        return pltpu.make_async_copy(wu_hbm.at[at, pl.ds(first, units)], wu.at[step], w_sem.at[1])
-
-    def down_copy(step):
-        at = pl.ds(pl.multiple_of(step * out_chunk, out_chunk), out_chunk)
-        return pltpu.make_async_copy(wd_hbm.at[pl.ds(first, units), at], wd.at[step], w_sem.at[2])
-
-    @pl.loop(0, k_steps)
-    def _(step):
-        gate_copy(step).start(priority=1)
-        up_copy(step).start(priority=1)
-
-    @pl.loop(0, j_steps)
-    def _(step):
-        down_copy(step).start(priority=1)
-
-    acc_g[...] = jnp.zeros_like(acc_g)
-    acc_u[...] = jnp.zeros_like(acc_u)
+    mine = pl.ds(first, units)
+    for i in range(LOADS):
+        at = pl.ds(i * (features // LOADS), features // LOADS)
+        pltpu.make_async_copy(
+            wg_hbm.at[at, mine], w.at[at, pl.ds(0, units)], w_sem.at[0]
+        ).start(priority=1)
+        pltpu.make_async_copy(
+            wu_hbm.at[at, mine], w.at[at, pl.ds(units, units)], w_sem.at[0]
+        ).start(priority=1)
+    for i in range(LOADS):
+        at = pl.ds(i * (units // LOADS), units // LOADS)
+        pltpu.make_async_copy(
+            wd_hbm.at[pl.ds(pl.multiple_of(first + i * (units // LOADS), 128), units // LOADS), :],
+            wd.at[at, :],
+            w_sem.at[1],
+        ).start(priority=1)
+
     for load in loads:
         load.wait()
     attend(q_ref, fk_ref, fv_ref, k_buf, v_buf, ctx_ref, q_rows, residual)
@@ -183,18 +172,17 @@
     residual[...] = full
     factor = lax.rsqrt(jnp.mean(full * full, axis=1, keepdims=True) + norm_eps)
     normed = (full * factor * gain_ref[...]).astype(jnp.bfloat16)
-    for k in range(k_steps):
-        xs[k] = normed[:, k * chunk : (k + 1) * chunk]
+    for k, (start, size) in enumerate(in_parts):
+        xs[k][...] = normed[:, start : start + size]
 
     pl.semaphore_wait(barrier, chips)
 
-    @pl.loop(0, k_steps)
-    def _(k):
+    for k in range(ins):
         for _, device in targets:
             pltpu.make_async_remote_copy(
-                src_ref=xs.at[k],
-                dst_ref=xd.at[k, chip],
-                send_sem=x_send.at[0],
+                src_ref=xs[k],
+                dst_ref=xd[k].at[chip],
+                send_sem=x_send.at[k],
                 recv_sem=x_recv.at[k],
                 device_id=device,
                 device_id_type=MESH,
@@ -205,42 +193,44 @@
 
     def forward(k):
         return pltpu.make_async_remote_copy(
-            src_ref=xd.at[k],
-            dst_ref=xf.at[k],
-            send_sem=f_send.at[0],
+            src_ref=xd[k],
+            dst_ref=xf[k],
+            send_sem=f_send.at[k],
             recv_sem=f_recv.at[k],
             device_id=partner,
             device_id_type=MESH,
         )
 
     def pass_on(k):
-        wait_for(xd.at[k], x_recv.at[k])
+        wait_for(xd[k], x_recv.at[k])
         forward(k).start()
 
     pass_on(0)
-    for k in range(k_steps):
-        if k + 1 < k_steps:
+    for k, (start, size) in enumerate(in_parts):
+        if k + 1 < ins:
             pass_on(k + 1)
         forward(k).wait_recv()
-        x32 = x32s.at[k % 2]
+        x32 = x32s[k]
         for q in range(chips):
-            x32[reqs * q : reqs * (q + 1), :] = xd[k, q].astype(jnp.float32)
-            x32[rows + reqs * q : rows + reqs * (q + 1), :] = xf[k, q].astype(jnp.float32)
+            x32[reqs * q : reqs * (q + 1), :] = xd[k][q].astype(jnp.float32)
+            x32[rows + reqs * q : rows + reqs * (q + 1), :] = xf[k][q].astype(jnp.float32)
         x = x32[...].astype(jnp.bfloat16)
         if k == 0:
-            wait_for(wg, w_sem.at[0])
-            wait_for(wu, w_sem.at[1])
-        acc_g[...] += jnp.dot(x, wg[k], preferred_element_type=jnp.float32)
-        acc_u[...] += jnp.dot(x, wu[k], preferred_element_type=jnp.float32)
-
-    gate = acc_g[...]
-    hidden[...] = (gate / (1.0 + jnp.exp(-gate)) * acc_u[...]).astype(jnp.bfloat16)
+            wait_for(w, w_sem.at[0])
+        term = jnp.dot(x, w[start : start + size, :], preferred_element_type=jnp.float32)
+        if k == 0:
+            acc[...] = term
+        else:
+            acc[...] += term
+
+    gate = acc[:, 0:units]
+    hidden[...] = (gate / (1.0 + jnp.exp(-gate)) * acc[:, units:]).astype(jnp.bfloat16)
 
     def give(j):
         return pltpu.make_async_remote_copy(
-            src_ref=ps.at[j],
-            dst_ref=pr.at[j],
-            send_sem=p_send.at[0],
+            src_ref=ps[j],
+            dst_ref=pr[j],
+            send_sem=p_send.at[j],
             recv_sem=p_recv.at[j],
             device_id=partner,
             device_id_type=MESH,
@@ -248,27 +238,30 @@
 
     def send_back(j):
         give(j).wait_recv()
-        both = (keep[j] + pr[j].astype(jnp.float32)).astype(jnp.bfloat16)
+        both = (keep[j][...] + pr[j][...].astype(jnp.float32)).astype(jnp.bfloat16)
         for q in range(chips):
-            ys[j, q] = both[reqs * q : reqs * (q + 1)]
-
-        for q, device in targets:
+            ys[j][q] = both[reqs * q : reqs * (q + 1)]
+
+        for q, device in owners:
             pltpu.make_async_remote_copy(
-                src_ref=ys.at[j, q],
-                dst_ref=yr.at[j, chip],
-                send_sem=y_send.at[0],
+                src_ref=ys[j].at[q],
+                dst_ref=yr[j].at[chip],
+                send_sem=y_send.at[j],
                 recv_sem=y_recv.at[j],
                 device_id=device,
                 device_id_type=MESH,
             ).start()
 
-    wait_for(wd, w_sem.at[2])
-    for j in range(j_steps + LAG):
-        if j < j_steps:
-            part = jnp.dot(hidden[...], wd[j], preferred_element_type=jnp.float32)
-            keep[j] = part[0:rows]
-            ps[j] = part[rows:].astype(jnp.bfloat16)
+    wait_for(wd, w_sem.at[1])
+    for j in range(outs + LAG):
+        if j < outs:
+            start, size = out_parts[j]
+            part = jnp.dot(
+                hidden[...], wd[:, start : start + size], preferred_element_type=jnp.float32
+            )
+            ps[j][...] = part[rows:].astype(jnp.bfloat16)
             give(j).start()
+            keep[j][...] = part[0:rows]
         if j >= LAG:
             send_back(j - LAG)
 
@@ -279,23 +272,25 @@
     for expert in range(EXPERTS):
         weights.append(jnp.sum(jnp.where(ids == expert, gates, 0.0), axis=1, keepdims=True))
 
-    for j in range(j_steps):
-        cols = slice(j * out_chunk, (j + 1) * out_chunk)
-        wait_for(yr.at[j], y_recv.at[j])
+    for j, (start, size) in enumerate(out_parts):
+        cols = slice(start, start + size)
+        wait_for(yr[j], y_recv.at[j])
         total = residual[:, cols]
         for expert in range(EXPERTS):
             share = None
             for group in range(groups):
                 for i in range(per_expert):
-                    term = yr[j, group * per_group + expert * per_expert + i].astype(jnp.float32)
+                    term = yr[j][group * per_group + expert * per_expert + i].astype(jnp.float32)
                     share = term if share is None else share + term
             total = total + weights[expert] * share
         out_ref[:, cols] = total.astype(out_ref.dtype)
 
-    wait_for(xd, x_send.at[0])
-    wait_for(xd, f_send.at[0])
-    wait_for(ps, p_send.at[0])
-    wait_for(ys, y_send.at[0])
+    for k in range(ins):
+        wait_for(xd[k], x_send.at[k])
+        forward(k).wait_send()
+    for j in range(outs):
+        give(j).wait_send()
+        wait_for(ys[j], y_send.at[j])
 
 
 def shared_local(
@@ -318,7 +313,8 @@
     units = gate_weight.shape[1] // groups
     chips = groups * n // 2
     rows = chips * reqs
-    k_steps, j_steps = features // IN_CHUNK, features // OUT_CHUNK
+    in_sizes = [size for _, size in cut(features, IN_SPLIT)]
+    out_sizes = [size for _, size in cut(features, OUT_SPLIT)]
     bf16, f32 = jnp.bfloat16, jnp.float32
     vmem = pl.BlockSpec(memory_space=pltpu.VMEM)
     hbm = pl.BlockSpec(memory_space=pltpu.HBM)
@@ -339,36 +335,28 @@
             pltpu.VMEM(expert_gates.shape, bf16),
             pltpu.VMEM(stored_keys.shape, bf16),
             pltpu.VMEM(stored_values.shape, bf16),
-            pltpu.VMEM((k_steps, IN_CHUNK, units), bf16),
-            pltpu.VMEM((k_steps, IN_CHUNK, units), bf16),
-            pltpu.VMEM((j_steps, units, OUT_CHUNK), bf16),
+            pltpu.VMEM((features, 2 * units), bf16),
+            pltpu.VMEM((units, features), bf16),
             pltpu.VMEM((reqs * features // HEAD_WIDTH, HEAD_WIDTH), f32),
             pltpu.VMEM((reqs, features), f32),
-            pltpu.VMEM((k_steps, reqs, IN_CHUNK), bf16),
-            pltpu.VMEM((k_steps, chips, reqs, IN_CHUNK), bf16),
-            pltpu.VMEM((k_steps, chips, reqs, IN_CHUNK), bf16),
-            pltpu.VMEM((2, 2 * rows, IN_CHUNK), f32),
-            pltpu.VMEM((2 * rows, units), f32),
-            pltpu.VMEM((2 * rows, units), f32),
+            pltpu.VMEM((2 * rows, 2 * units), f32),
             pltpu.VMEM((2 * rows, units), bf16),
-            pltpu.VMEM((j_steps, rows, OUT_CHUNK), f32),
-            pltpu.VMEM((j_steps, rows, OUT_CHUNK), bf16),
-            pltpu.VMEM((j_steps, rows, OUT_CHUNK), bf16),
-            pltpu.VMEM((j_steps, chips, reqs, OUT_CHUNK), bf16),
-            pltpu.VMEM((j_steps, chips, reqs, OUT_CHUNK), bf16),
+            *(pltpu.VMEM((reqs, size), bf16) for size in in_sizes),
+            *(pltpu.VMEM((chips, reqs, size), bf16) for size in in_sizes),
+            *(pltpu.VMEM((chips, reqs, size), bf16) for size in in_sizes),
+            *(pltpu.VMEM((2 * rows, size), f32) for size in in_sizes),
+            *(pltpu.VMEM((rows, size), f32) for size in out_sizes),
+            *(pltpu.VMEM((rows, size), bf16) for size in out_sizes),
+            *(pltpu.VMEM((rows, size), bf16) for size in out_sizes),
+            *(pltpu.VMEM((chips, reqs, size), bf16) for size in out_sizes),
+            *(pltpu.VMEM((chips, reqs, size), bf16) for size in out_sizes),
             dma((10,)),
-            dma((3,)),
-            dma((1,)),
-            dma((k_steps,)),
-            dma((1,)),
-            dma((k_steps,)),
-            dma((1,)),
-            dma((j_steps,)),
-            dma((1,)),
-            dma((j_steps,)),
+            dma((2,)),
+            *(dma((len(IN_SPLIT),)) for _ in range(4)),
+            *(dma((len(OUT_SPLIT),)) for _ in range(4)),
         ],
         compiler_params=pltpu.CompilerParams(
-            collective_id=0, has_side_effects=True, vmem_limit_bytes=SHARED_VMEM
+            collective_id=0, has_side_effects=True, vmem_limit_bytes=66_000_000
         ),
         name="decode_step",
     )(
@@ -673,7 +661,10 @@
 
     def local(*args):
         units = args[10].shape[1]
+        features = args[0].shape[1]
+        split = max(sum(IN_SPLIT), sum(OUT_SPLIT))
         shared = n % (2 * EXPERTS) == 0 and units % (128 * groups) == 0
+        shared = shared and features % (128 * split) == 0
         return (shared_local if shared else plain_local)(*args)
 
     return jax.shard_map(local, mesh=mesh, in_specs=in_specs, out_specs=out_specs, check_vma=False)

time: 29.5 us -> 28.9 us (0.980)
  Pallas kernels: 27.9 us -> 27.3 us
    pallas_call x1, Pallas kernels: 27.9 us -> 27.3 us  [shared_local(): pl.pallas_call(functools.partial(shared_kernel, groups, n), out_shape=jax...]
where the time goes in v3:
time: 28.9 us; the launch traced here: 28.7 us
  Pallas kernels  27.3 us (94%)
  local copies, waits for them, and re-layouts  1.34 us (5%)
    pallas_call x1, Pallas kernels, shared_local(): pl.pallas_call(functools.partial(shared_kernel, groups, n), out_shape=jax...  27.3 us
    unnamed x1, local copies, waits for them, and re-layouts  1.34 us

profile of v3, /device:TPU:0, one launch (start us, length us, event | category | flops | bytes accessed | tf_op | source)
XLA Modules:
  0.0 28.7 jit_solution(18390311867618275467)
XLA Ops:
  0.0 27.3 %decode_step.1 = bf16[2,4096]{1,0:T(2,128)(2,1)} custom-call(s32[2]{0:T(128)} %refs_0_.1, bf16[2,4096]{1,0:T(2,128)(2,1)} %refs_1_.1, bf16[2,4096]{1,0:T(2,128)(2,1)} %refs_2_.1, bf16[2,512]{1,0:T(2,128)(2,1)} %refs_3_.1, bf16[2,512]{1,0:T(2,128)(2,1)} %refs_4_.1, f32[1,4096]{1,0:T(1,128)} %bitcast.1, s32[2,2]{1,0:T(2,128)} %refs_6_.1, ...), custom_call_target="tpu_custom_call" | custom-call | tf_op jit(solution)/shard_map/decode_step/pallas_call | solution.py:322
  27.3 1.3 %copy.15 = bf16[2,4096]{1,0:T(2,128)(2,1)} copy(bf16[2,4096]{1,0:T(2,128)(2,1)} %decode_step.1) | data formatting | bytes 32768
